TPU v7x, 32 devices: a whole 2x2x4 slice. The times are simulated.
32 devices in a mesh: path: 8 (over y, x, core), mod: 4 (over z).
Axes of the slice: x: 2, y: 2, z: 4, core: 2. Of those that a mesh axis runs over, the one named last changes fastest.
Arguments:
- activations: bfloat16 [8, 512, 4096], P('path', 'mod'), may hold values from -6 to 6
- cotangent: bfloat16 [8, 512, 4096], P('path', 'mod'), may hold values from -6 to 6
- first_weight: bfloat16 [8, 4096, 4096], P('path', None, 'mod'), may hold values from -6 to 6
- second_weight: bfloat16 [8, 4096, 4096], P('path', None, 'mod'), may hold values from -6 to 6
- first_master: float32 [4, 4096, 4096], P(None, ('path', 'mod')), may hold values from -6 to 6
- second_master: float32 [4, 4096, 4096], P(None, ('path', 'mod')), may hold values from -6 to 6
- first_moment: float32 [4, 4096, 4096], P(None, ('path', 'mod')), may hold values from -3 to 3
- second_moment: float32 [4, 4096, 4096], P(None, ('path', 'mod')), may hold values from -3 to 3
- routing: int32 [8, 2], replicated, may hold values from 0 to 3, as said below
Outputs:
- first_result: bfloat16 [8, 4096, 4096], P('path', None, 'mod')
- second_result: bfloat16 [8, 4096, 4096], P('path', None, 'mod')
Inputs may be any that keep to these rules, and one draw needn't show every extreme that they name: `routing`: for each of the two levels, every one of the 4 modules is taken by at least one path.
All inputs are finite; a program needn't handle non-finite values.
Results may differ from a plain program's by a relative error of at most 0.0045.
Values may be sent and summed in bfloat16 or wider, within the bound.
A program may use at most 192 MiB of HBM per device.

v0:
```python
import jax
import jax.numpy as jnp
from jax import lax
from jax.sharding import PartitionSpec as P

inner_rate = 1.0
outer_rate = 0.7
momentum_decay = 0.9


def to_owners(stacked, onehot):
    level_count = stacked.shape[0]
    columns = stacked.shape[2]
    path_count = onehot.shape[1]
    groups = lax.axis_size("mod")
    arrived = lax.all_to_all(stacked, ("path", "mod"), split_axis=1, concat_axis=2, tiled=True)
    owned_rows = arrived.shape[1]
    arrived = arrived.reshape(level_count, owned_rows, path_count, groups, columns)
    summed = jnp.einsum("lrpkc,lpm->lmrkc", arrived, onehot, preferred_element_type=jnp.float32)
    return summed.reshape(level_count, onehot.shape[2], owned_rows, groups * columns)


def outer_step(summed, onehot, master, moment):
    path_total = jnp.sum(onehot.astype(jnp.float32), axis=1)[:, :, None, None]
    outer = master - summed / path_total
    moment_new = momentum_decay * moment + outer
    return (master - outer_rate * (outer + momentum_decay * moment_new)).astype(jnp.bfloat16)


def to_paths(renewed, onehot):
    level_count, module_count, owned_rows, model_width = renewed.shape
    groups = lax.axis_size("mod")
    path_count = onehot.shape[1]
    columns = model_width // groups
    split = renewed.reshape(level_count, module_count, owned_rows, groups, columns)
    chosen = jnp.einsum(
        "lmrkc,lpm->lrpkc", split, onehot, preferred_element_type=jnp.float32
    ).astype(jnp.bfloat16)
    outgoing = chosen.reshape(level_count, owned_rows, path_count * groups * columns)
    return lax.all_to_all(outgoing, ("path", "mod"), split_axis=2, concat_axis=1, tiled=True)


def body(
    activations,
    cotangent,
    first_weight,
    second_weight,
    first_master,
    second_master,
    first_moment,
    second_moment,
    routing,
):
    inputs_full, upstream = (
        lax.all_gather(activations, "mod", axis=1, tiled=True),
        lax.all_gather(cotangent, "mod", axis=1, tiled=True),
    )
    inputs_full = inputs_full[0]
    upstream = upstream[0]
    weight_in = first_weight[0]
    weight_out = second_weight[0]
    scale = inputs_full.shape[1] ** (-0.5)
    pre = jnp.dot(inputs_full, weight_in, preferred_element_type=jnp.float32) * scale
    hidden = jax.nn.silu(pre).astype(jnp.bfloat16)
    grad_hidden = jnp.dot(upstream, weight_out, preferred_element_type=jnp.float32) * scale
    grad_out = (
        lax.dot_general(
            upstream, hidden, (((0,), (0,)), ((), ())), preferred_element_type=jnp.float32
        )
        * scale
    )
    trained_out = (weight_out.astype(jnp.float32) - inner_rate * grad_out).astype(jnp.bfloat16)
    sigma = jax.nn.sigmoid(pre)
    grad_pre = (grad_hidden * sigma * (1.0 + pre * (1.0 - sigma))).astype(jnp.bfloat16)
    grad_in = (
        lax.dot_general(
            inputs_full, grad_pre, (((0,), (0,)), ((), ())), preferred_element_type=jnp.float32
        )
        * scale
    )
    trained_in = (weight_in.astype(jnp.float32) - inner_rate * grad_in).astype(jnp.bfloat16)
    module_count = first_master.shape[0]
    module_ids = jnp.arange(module_count)
    onehot = (jnp.transpose(routing)[:, :, None] == module_ids[None, None, :]).astype(jnp.bfloat16)
    summed = to_owners(jnp.stack((trained_in, trained_out)), onehot)
    renewed = outer_step(
        summed,
        onehot,
        jnp.stack((first_master, second_master)),
        jnp.stack((first_moment, second_moment)),
    )
    returned = to_paths(renewed, onehot)
    first_back = returned[0]
    second_back = returned[1]
    return (first_back[None], second_back[None])


def solution(mesh):
    return jax.shard_map(
        body,
        mesh=mesh,
        in_specs=(
            P("path", "mod", None),
            P("path", "mod", None),
            P("path", None, "mod"),
            P("path", None, "mod"),
            P(None, ("path", "mod"), None),
            P(None, ("path", "mod"), None),
            P(None, ("path", "mod"), None),
            P(None, ("path", "mod"), None),
            P(),
        ),
        out_specs=(P("path", None, "mod"), P("path", None, "mod")),
        check_vma=False,
    )
```

profile of v0, /device:TPU:1, one launch (start us, length us, event | category | flops | bytes accessed | tf_op | source)
XLA Modules:
  0.0 1153.4 jit_solution(4697887328991194632)
XLA Ops:
  8.6 12.0 %copy.45 = bf16[1,4096,1024]{1,2,0:T(8,128)(2,1)} copy(bf16[1,4096,1024]{2,1,0:T(8,128)(2,1)} %param.11) | data formatting | bytes 16777216 | tf_op args[2]
  20.6 11.9 %copy.46 = bf16[1,4096,1024]{1,2,0:T(8,128)(2,1)} copy(bf16[1,4096,1024]{2,1,0:T(8,128)(2,1)} %param.12) | data formatting | bytes 16777216 | tf_op args[3]
  32.6 59.7 %all-gather.5.cloned.1.call-done = bf16[1,512,4096]{2,1,0:T(8,128)(2,1)} async-done(((bf16[1,128,4096]{2,1,0:T(8,128)(2,1)}), bf16[1,512,4096]{2,1,0:T(8,128)(2,1)}) %all-gather.5.cloned.1.call-update) | async-done | bytes 4194320 | tf_op jit(solution)/shard_map/all_gather | solution.py:55
  100.4 72.7 %all-gather.3.cloned.1.call-done = bf16[1,512,4096]{2,1,0:T(8,128)(2,1)} async-done(((bf16[1,128,4096]{2,1,0:T(8,128)(2,1)}), bf16[1,512,4096]{2,1,0:T(8,128)(2,1)}) %all-gather.3.cloned.1.call-update) | async-done | bytes 4194320 | tf_op jit(solution)/shard_map/all_gather | solution.py:56
  173.1 18.0 %fusion.18 = bf16[1,4096,1024]{1,2,0:T(8,128)(2,1)} fusion(bf16[1,4096,1024]{1,2,0:T(8,128)(2,1)} %copy.45, bf16[1,512,4096]{2,1,0:T(8,128)(2,1)} %all-gather.5.cloned.1.call-done, f32[512,1024]{1,0:T(8,128)S(1)} %fusion.14, bf16[1,4096,1024]{2,1,0:T(8,128)(2,1)} %param.12, bf16[1,512,4096]{2,1,0:T(8,128)(2,1)} %all-gather.3.cloned.1.call-done), kind=kOutput, calls=%fused_computation.21 | convolution fusion | flops 8612478976 | bytes 35651584 | tf_op jit(solution)/shard_map/dot_general | solution.py:76
  191.1 11.1 fusion.19
  202.1 10.5 pad_maximum_fusion.1
  212.6 41.5 %copy.47 = bf16[2,4096,1024]{2,0,1:T(2,128)(2,1)} copy(bf16[2,4096,1024]{1,2,0:T(8,128)(2,1)} %pad_maximum_fusion.1) | data formatting | bytes 33554432 | tf_op jit(solution)/shard_map/stack | solution.py:85
  258.4 8.9 copy.41
  267.3 10.4 copy.43
  277.7 8.9 copy.42
  286.6 10.3 copy.44
  305.8 10.4 copy.52
  316.2 8.9 copy.51
  325.0 10.3 copy.53
  335.4 280.1 %all-to-all-done = bf16[2,4096,1024]{2,0,1:T(2,128)(2,1)} async-done(((bf16[2,4096,1024]{2,0,1:T(2,128)(2,1)}), bf16[2,4096,1024]{2,0,1:T(2,128)(2,1)}, u32[]{:S(2)}, u32[]{:S(2)}) %all-to-all-start) | async-done | bytes 16777248 | tf_op jit(solution)/shard_map/all_to_all | solution.py:16
  615.5 16.4 %copy.48 = bf16[2,4096,1024]{2,1,0:T(8,128)(2,1)} copy(bf16[2,4096,1024]{2,0,1:T(2,128)(2,1)} %all-to-all-done) | data formatting | bytes 33554432 | tf_op jit(solution)/shard_map/all_to_all | solution.py:16
  632.0 40.2 %convert_bitcast_fusion = bf16[2,128,8,4,1024]{4,2,3,1,0:T(8,128)(2,1)} fusion(f32[1,4,128,4,1024]{4,1,3,2,0:T(4,128)} %copy.53, f32[1,4,128,4,1024]{4,1,3,2,0:T(4,128)} %copy.52, bf16[2,128,8,4,1024]{4,1,3,2,0:T(8,128)(2,1)} %bitcast.86, f32[1,4,128,4,1024]{4,1,3,2,0:T(4,128)} %copy.44, f32[1,4,128,4,1024]{4,1,3,2,0:T(4,128)} %copy.43, ...), kind=kOutput, calls=%fused_computation.15 | convolution fusion | flops 188743808 | bytes 67108960 | tf_op jit(solution)/shard_map/lmrkc,lpm->lrpkc/dot_general | solution.py:36
  672.2 23.0 %copy.54 = bf16[2,128,8,4,1024]{1,4,3,2,0:T(8,128)(2,1)} copy(bf16[2,128,8,4,1024]{4,2,3,1,0:T(8,128)(2,1)} %convert_bitcast_fusion) | data formatting | bytes 33554432 | tf_op jit(solution)/shard_map/convert_element_type | solution.py:38
  695.2 30.0 %copy.55 = bf16[2,128,32768]{1,0,2:T(2,128)(2,1)S(1)} copy(bf16[2,128,32768]{1,2,0:T(8,128)(2,1)} %bitcast.81) | data formatting | bytes 33554432 | tf_op jit(solution)/shard_map/reshape | solution.py:39
  725.2 381.5 %all_to_all.30 = bf16[2,128,32768]{1,0,2:T(2,128)(2,1)} all-to-all(bf16[2,128,32768]{1,0,2:T(2,128)(2,1)S(1)} %copy.55), channel_id=1, replica_groups=mesh['path'=8,'mod'=4] {'path','mod'}, dimensions={2} | all-to-all | bytes 33554432 | tf_op jit(solution)/shard_map/all_to_all | solution.py:40
  1106.8 9.6 copy.56
  1122.7 11.9 %copy.57 = bf16[1,32,128,1024]{3,2,1,0:T(8,128)(2,1)} copy(bf16[1,32,128,1024]{2,3,1,0:T(8,128)(2,1)} %get-tuple-element.3) | data formatting | bytes 16777216 | tf_op jit(solution)/shard_map/slice | solution.py:93
  1134.6 11.9 %copy.58 = bf16[1,32,128,1024]{3,2,1,0:T(8,128)(2,1)} copy(bf16[1,32,128,1024]{2,3,1,0:T(8,128)(2,1)} %get-tuple-element.2) | data formatting | bytes 16777216 | tf_op jit(solution)/shard_map/slice | solution.py:94
  (13 shorter events, 29.1 us)
Async XLA Ops:
  7.2 85.1 %all-gather.5.cloned.1.call-start = ((), (), s32[]{:S(2)}) async-start(), calls=%async_computation.3 | async-start | bytes 5242880 | tf_op jit(solution)/shard_map/all_gather | solution.py:55
  7.9 165.2 %all-gather.3.cloned.1.call-start = ((), (), s32[]{:S(2)}) async-start(), calls=%async_computation.2 | async-start | bytes 5242880 | tf_op jit(solution)/shard_map/all_gather | solution.py:56
  191.1 11.1 copy-start
  254.1 361.4 %all-to-all-start = ((bf16[2,4096,1024]{2,0,1:T(2,128)(2,1)}), bf16[2,4096,1024]{2,0,1:T(2,128)(2,1)}, u32[]{:S(2)}, u32[]{:S(2)}) async-start(bf16[2,4096,1024]{2,0,1:T(2,128)(2,1)} %copy.47), calls=%async_computation | async-start | bytes 33554432 | tf_op jit(solution)/shard_map/all_to_all | solution.py:16
  325.0 10.3 copy-start.1
Sparse Core Ops, SparseCore 0:
  9.5 82.6 all-gather.4
  93.8 79.2 all-gather.2
where the time goes:
time: 1160 us; the launch traced here: 1150 us
  waiting for transfers between devices  414 us (36%)
  blocking collectives  382 us (33%)
  local copies, waits for them, and re-layouts  252 us (22%)
  matrix products  77.4 us (7%)
  between operations  14.1 us (1%)
    all_to_all x1, blocking collectives, to_paths(): lax.all_to_all(outgoing, ('path', 'mod'), split_axis=2, concat_axis=1, ti...  382 us
    all_to_all x1, waiting for transfers between devices, to_owners(): lax.all_to_all(stacked, ('path', 'mod'), split_axis=1, concat_axis=2, til...  280 us
    all_gather x1, waiting for transfers between devices, body(): lax.all_gather(cotangent, 'mod', axis=1, tiled=True)  72.7 us
    all_gather x1, waiting for transfers between devices, body(): lax.all_gather(activations, 'mod', axis=1, tiled=True)  59.7 us
    unnamed x10, local copies, waits for them, and re-layouts  59.5 us
    another operation x1, local copies, waits for them, and re-layouts, body(): summed = to_owners(jnp.stack((trained_in, trained_out)), onehot)  41.5 us
    dot_general x1, matrix products, to_paths(): jnp.einsum('lmrkc,lpm->lrpkc', split, onehot, preferred_element_type=jnp....  40.2 us
    reshape x1, local copies, waits for them, and re-layouts, to_paths(): chosen.reshape(level_count, owned_rows, path_count * groups * columns)  30 us
  transfers between devices with their start and end apart: 3, of which 3 were waited for; matrix products, arithmetic and copies ran while one was open for 9% of the time, Pallas kernels for 0%

commit v1 on v0

--- a/solution.py
+++ b/solution.py
@@ -6,6 +6,13 @@
 inner_rate = 1.0
 outer_rate = 0.7
 momentum_decay = 0.9
+
+
+def swap_blocks(x, axis, split, join):
+    peers = lax.axis_size(axis)
+    blocks = jnp.stack(jnp.split(x, peers, axis=split), axis=0)
+    blocks = lax.all_to_all(blocks, axis, split_axis=0, concat_axis=0)
+    return jnp.concatenate(blocks, axis=join)
 
 
 def to_owners(stacked, onehot):
@@ -37,7 +44,7 @@
         "lmrkc,lpm->lrpkc", split, onehot, preferred_element_type=jnp.float32
     ).astype(jnp.bfloat16)
     outgoing = chosen.reshape(level_count, owned_rows, path_count * groups * columns)
-    return lax.all_to_all(outgoing, ("path", "mod"), split_axis=2, concat_axis=1, tiled=True)
+    return swap_blocks(outgoing, ("path", "mod"), 2, 1)
 
 
 def body(

time: 1160 us -> 1140 us (0.983)
  local copies, waits for them, and re-layouts: 252 us -> 232 us
    reshape x1 -> x0, local copies, waits for them, and re-layouts: 30 us -> none  [to_paths(): chosen.reshape(level_count, owned_rows, path_count * groups * columns)]
    unnamed x10 -> x43, local copies, waits for them, and re-layouts: 59.5 us -> 79.5 us
  transfers between devices with their start and end apart: 3 -> 3, of which waited for: 3 -> 3; matrix products, arithmetic and copies ran while one was open for 9% -> 10% of each run, Pallas kernels for 0% -> 0%
where the time goes in v1:
time: 1140 us; the launch traced here: 1130 us
  waiting for transfers between devices  414 us (36%)
  blocking collectives  381 us (33%)
  local copies, waits for them, and re-layouts  232 us (20%)
  matrix products  77.4 us (7%)
  between operations  14.2 us (1%)
    all_to_all x1, blocking collectives, swap_blocks(): blocks = lax.all_to_all(blocks, axis, split_axis=0, concat_axis=0)  381 us
    all_to_all x1, waiting for transfers between devices, to_owners(): lax.all_to_all(stacked, ('path', 'mod'), split_axis=1, concat_axis=2, til...  280 us
    unnamed x43, local copies, waits for them, and re-layouts  79.5 us
    all_gather x1, waiting for transfers between devices, body(): lax.all_gather(cotangent, 'mod', axis=1, tiled=True)  72.7 us
    all_gather x1, waiting for transfers between devices, body(): lax.all_gather(activations, 'mod', axis=1, tiled=True)  59.7 us
    another operation x1, local copies, waits for them, and re-layouts, body(): summed = to_owners(jnp.stack((trained_in, trained_out)), onehot)  41.6 us
    dot_general x1, matrix products, to_paths(): jnp.einsum('lmrkc,lpm->lrpkc', split, onehot, preferred_element_type=jnp....  40.2 us
    convert_element_type x1, local copies, waits for them, and re-layouts, to_paths(): chosen = jnp.einsum('lmrkc,lpm->lrpkc', split, onehot, preferred_element_...  22.9 us
  transfers between devices with their start and end apart: 3, of which 3 were waited for; matrix products, arithmetic and copies ran while one was open for 10% of the time, Pallas kernels for 0%

profile of v1, /device:TPU:1, one launch (start us, length us, event | category | flops | bytes accessed | tf_op | source)
XLA Modules:
  0.0 1133.8 jit_solution(13769484524264929159)
XLA Ops:
  8.6 12.0 %copy.76 = bf16[1,4096,1024]{1,2,0:T(8,128)(2,1)} copy(bf16[1,4096,1024]{2,1,0:T(8,128)(2,1)} %param.11) | data formatting | bytes 16777216 | tf_op args[2]
  20.6 11.9 %copy.77 = bf16[1,4096,1024]{1,2,0:T(8,128)(2,1)} copy(bf16[1,4096,1024]{2,1,0:T(8,128)(2,1)} %param.12) | data formatting | bytes 16777216 | tf_op args[3]
  32.6 59.7 %all-gather.5.cloned.1.call-done = bf16[1,512,4096]{2,1,0:T(8,128)(2,1)} async-done(((bf16[1,128,4096]{2,1,0:T(8,128)(2,1)}), bf16[1,512,4096]{2,1,0:T(8,128)(2,1)}) %all-gather.5.cloned.1.call-update) | async-done | bytes 4194320 | tf_op jit(solution)/shard_map/all_gather | solution.py:62
  92.2 8.1 fusion.14
  100.4 72.7 %all-gather.3.cloned.1.call-done = bf16[1,512,4096]{2,1,0:T(8,128)(2,1)} async-done(((bf16[1,128,4096]{2,1,0:T(8,128)(2,1)}), bf16[1,512,4096]{2,1,0:T(8,128)(2,1)}) %all-gather.3.cloned.1.call-update) | async-done | bytes 4194320 | tf_op jit(solution)/shard_map/all_gather | solution.py:63
  173.1 18.0 %fusion.18 = bf16[1,4096,1024]{1,2,0:T(8,128)(2,1)} fusion(bf16[1,4096,1024]{1,2,0:T(8,128)(2,1)} %copy.76, bf16[1,512,4096]{2,1,0:T(8,128)(2,1)} %all-gather.5.cloned.1.call-done, f32[512,1024]{1,0:T(8,128)S(1)} %fusion.14, bf16[1,4096,1024]{2,1,0:T(8,128)(2,1)} %param.12, bf16[1,512,4096]{2,1,0:T(8,128)(2,1)} %all-gather.3.cloned.1.call-done), kind=kOutput, calls=%fused_computation.21 | convolution fusion | flops 8612478976 | bytes 35651584 | tf_op jit(solution)/shard_map/dot_general | solution.py:83
  191.1 11.1 fusion.19
  202.1 10.5 pad_maximum_fusion.1
  212.6 41.6 %copy.78 = bf16[2,4096,1024]{2,0,1:T(2,128)(2,1)} copy(bf16[2,4096,1024]{1,2,0:T(8,128)(2,1)} %pad_maximum_fusion.1) | data formatting | bytes 33554432 | tf_op jit(solution)/shard_map/stack | solution.py:92
  258.4 8.9 copy.72
  267.3 10.4 copy.74
  277.7 8.9 copy.73
  286.6 10.4 copy.75
  297.0 8.9 copy.81
  305.8 10.4 copy.83
  316.2 8.9 copy.82
  325.1 10.3 copy.84
  335.5 280.1 %all-to-all-done = bf16[2,4096,1024]{2,0,1:T(2,128)(2,1)} async-done(((bf16[2,4096,1024]{2,0,1:T(2,128)(2,1)}), bf16[2,4096,1024]{2,0,1:T(2,128)(2,1)}, u32[]{:S(2)}, u32[]{:S(2)}) %all-to-all-start) | async-done | bytes 16777248 | tf_op jit(solution)/shard_map/all_to_all | solution.py:23
  615.6 16.4 %copy.79 = bf16[2,4096,1024]{2,1,0:T(8,128)(2,1)} copy(bf16[2,4096,1024]{2,0,1:T(2,128)(2,1)} %all-to-all-done) | data formatting | bytes 33554432 | tf_op jit(solution)/shard_map/all_to_all | solution.py:23
  632.0 40.2 %convert_bitcast_fusion = bf16[2,128,8,4,1024]{4,2,3,1,0:T(8,128)(2,1)} fusion(f32[1,4,128,4,1024]{4,1,3,2,0:T(4,128)} %copy.84, f32[1,4,128,4,1024]{4,1,3,2,0:T(4,128)} %copy.83, bf16[2,128,8,4,1024]{4,1,3,2,0:T(8,128)(2,1)} %bitcast.243, f32[1,4,128,4,1024]{4,1,3,2,0:T(4,128)} %copy.75, f32[1,4,128,4,1024]{4,1,3,2,0:T(4,128)} %copy.74, ...), kind=kOutput, calls=%fused_computation.15 | convolution fusion | flops 188743808 | bytes 67108960 | tf_op jit(solution)/shard_map/lmrkc,lpm->lrpkc/dot_general | solution.py:43
  672.2 22.9 %copy.85 = bf16[2,128,8,4,1024]{1,4,3,2,0:T(8,128)(2,1)} copy(bf16[2,128,8,4,1024]{4,2,3,1,0:T(8,128)(2,1)} %convert_bitcast_fusion) | data formatting | bytes 33554432 | tf_op jit(solution)/shard_map/convert_element_type | solution.py:45
  715.4 381.4 %all_to_all.20 = bf16[32,2,128,1024]{2,3,1,0:T(8,128)(2,1)S(1)} all-to-all(bf16[32,2,128,1024]{2,3,1,0:T(8,128)(2,1)S(1)} %fusion.38), channel_id=1, replica_groups=mesh['path'=8,'mod'=4] {'path','mod'}, dimensions={0} | all-to-all | bytes 33554432 | tf_op jit(solution)/shard_map/all_to_all | solution.py:14
  1103.1 11.9 %copy.86 = bf16[1,32,128,1024]{3,2,1,0:T(8,128)(2,1)} copy(bf16[1,32,128,1024]{2,3,0,1:T(8,128)(2,1)} %get-tuple-element.3) | data formatting | bytes 16777216 | tf_op jit(solution)/shard_map/slice | solution.py:100
  1115.0 11.9 %copy.87 = bf16[1,32,128,1024]{3,2,1,0:T(8,128)(2,1)} copy(bf16[1,32,128,1024]{2,3,0,1:T(8,128)(2,1)} %get-tuple-element.2) | data formatting | bytes 16777216 | tf_op jit(solution)/shard_map/slice | solution.py:101
  (45 shorter events, 32.2 us)
Async XLA Ops:
  7.2 85.1 %all-gather.5.cloned.1.call-start = ((), (), s32[]{:S(2)}) async-start(), calls=%async_computation.3 | async-start | bytes 5242880 | tf_op jit(solution)/shard_map/all_gather | solution.py:62
  7.9 165.2 %all-gather.3.cloned.1.call-start = ((), (), s32[]{:S(2)}) async-start(), calls=%async_computation.2 | async-start | bytes 5242880 | tf_op jit(solution)/shard_map/all_gather | solution.py:63
  191.1 11.1 copy-start.1
  254.2 361.4 %all-to-all-start = ((bf16[2,4096,1024]{2,0,1:T(2,128)(2,1)}), bf16[2,4096,1024]{2,0,1:T(2,128)(2,1)}, u32[]{:S(2)}, u32[]{:S(2)}) async-start(bf16[2,4096,1024]{2,0,1:T(2,128)(2,1)} %copy.78), calls=%async_computation | async-start | bytes 33554432 | tf_op jit(solution)/shard_map/all_to_all | solution.py:23
  316.2 19.2 %copy-start.2 = (s32[8,2]{0,1:T(2,128)S(1)}, s32[8,2]{0,1:T(2,128)}, u32[]{:S(2)}) copy-start(s32[8,2]{0,1:T(2,128)} %param.17) | copy-start | bytes 196
  695.1 19.0 %copy-start = (bf16[2,128,8,4,1024]{1,4,3,2,0:T(8,128)(2,1)S(1)}, bf16[2,128,8,4,1024]{1,4,3,2,0:T(8,128)(2,1)}, u32[]{:S(2)}) copy-start(bf16[2,128,8,4,1024]{1,4,3,2,0:T(8,128)(2,1)} %copy.85) | copy-start | bytes 50331652
Sparse Core Ops, SparseCore 0:
  9.5 82.6 all-gather.4
  93.8 79.2 all-gather.2
